TPU v7x, 256 devices: a whole 4x4x8 slice. The times are simulated.
256 devices in a mesh: batch: 8 (over x, z_hi), seq: 4 (over y), mp: 8 (over z_lo, core).
Axes of the slice: x: 4, y: 4, z: 8 (z_hi: 2, z_lo: 4; z = z_hi * 4 + z_lo), core: 2. Of those that a mesh axis runs over, the one named last changes fastest.
Arguments:
- context: bfloat16 [4096, 6144], P(('batch', 'seq'), 'mp'), may hold values from -0.1875 to 0.1875
- cotangent: bfloat16 [4096, 6144], P(('batch', 'seq'), 'mp'), may hold values from -6 to 6
- out_weight: bfloat16 [6144, 6144], P(None, 'mp'), may hold values from -0.078125 to 0.078125
Outputs:
- grad_weight: float32 [6144, 6144], P(('batch', 'seq'), 'mp')
- grad_context: bfloat16 [4096, 6144], P(('batch', 'seq'), 'mp')
All inputs are finite; a program needn't handle non-finite values.
Results may differ from a plain program's by a relative error of at most 0.001.
Values may be sent and summed in bfloat16 or wider, within the bound.
No kernel may reach another device: no remote copies, remote signals or barrier semaphores. Data moves between devices by JAX's collectives and lax.ppermute only.
A program may use at most 64 MiB of HBM per device.

v0:
```python
import jax
import jax.numpy as jnp
from jax import lax
from jax.sharding import PartitionSpec as P


def joined_along(blocks, dim):
    dims = list(blocks.shape[1:])
    dims[dim] *= blocks.shape[0]
    return jnp.moveaxis(blocks, 0, dim).reshape(dims)


def copy_for_each(array, axis):
    copies = jnp.broadcast_to(array, (lax.axis_size(axis), *array.shape))
    return lax.all_to_all(copies, axis, split_axis=0, concat_axis=0, tiled=True)


def gathered_copies(array, axis, dim):
    return joined_along(copy_for_each(array, axis), dim)


def shards(context, cotangent, out_weight):
    groups = lax.axis_size(("batch", "seq"))
    members = lax.axis_size("mp")
    split_rows = lax.all_to_all(context, "mp", split_axis=0, concat_axis=1, tiled=True)
    block_rows = lax.all_to_all(
        split_rows, ("batch", "seq"), split_axis=1, concat_axis=0, tiled=True
    )
    feature_block = gathered_copies(block_rows, "mp", 0)
    all_cotangent = lax.all_gather(cotangent, ("batch", "seq"), axis=0, tiled=True)
    share = split_rows.shape[0]
    shaped_context = feature_block.reshape(members, groups, share, feature_block.shape[1])
    shaped_cotangent = all_cotangent.reshape(groups, members, share, all_cotangent.shape[1])
    grad_weight = lax.dot_general(
        shaped_context,
        shaped_cotangent,
        (((0, 1, 2), (1, 0, 2)), ((), ())),
        preferred_element_type=jnp.float32,
    )
    partial_input = lax.dot_general(
        cotangent, out_weight, (((1,), (1,)), ((), ())), preferred_element_type=jnp.float32
    )
    grad_context = lax.psum_scatter(partial_input, "mp", scatter_dimension=1, tiled=True).astype(
        jnp.bfloat16
    )
    return (grad_weight, grad_context)


def solution(mesh):
    return jax.shard_map(
        shards,
        mesh=mesh,
        in_specs=(P(("batch", "seq"), "mp"), P(("batch", "seq"), "mp"), P(None, "mp")),
        out_specs=(P(("batch", "seq"), "mp"), P(("batch", "seq"), "mp")),
        check_vma=False,
    )
```

profile of v0, /device:TPU:1, one launch (start us, length us, event | category | flops | bytes accessed | tf_op | source)
XLA Modules:
  0.0 193.0 jit_solution(11909060434958061613)
XLA Ops:
  8.0 0.0 copy-start
  8.0 0.0 reduce-scatter.2.cloned.1.call-start
  8.1 8.6 %fusion.5 = f32[128,6144]{1,0:T(8,128)} fusion(bf16[128,768]{1,0:T(8,128)(2,1)} %param.4, bf16[6144,768]{1,0:T(8,128)(2,1)} %param.5), kind=kOutput, calls=%fused_computation.3 | convolution fusion | flops 1207959552 | bytes 12779520 | tf_op jit(solution)/shard_map/dot_general | solution.py:40
  16.7 0.0 reduce-scatter.2.cloned.1.call-update
  16.7 0.0 all-gather.2.cloned.1.call-start
  16.7 0.5 all-gather.2.cloned.1.call-update
  17.3 0.0 copy-done
  17.3 13.7 %all_to_all.40 = bf16[8,16,768]{2,1,0:T(8,128)(2,1)S(1)} all-to-all(bf16[8,16,768]{2,1,0:T(8,128)(2,1)S(1)} %bitcast.17), channel_id=1, replica_groups=mesh['batch'=8,'seq'=4,'mp'=8] {'mp'}, dimensions={0} | all-to-all | bytes 393216 | tf_op jit(solution)/shard_map/all_to_all | solution.py:25
  31.0 0.1 copy.9
  31.1 0.3 all_to_all.32
  31.3 0.2 copy.10
  31.5 28.9 %all_to_all.41 = bf16[16,32,192]{2,0,1:T(8,128)(2,1)S(1)} all-to-all(bf16[16,32,192]{2,0,1:T(8,128)(2,1)S(1)} %copy.10), channel_id=1, replica_groups=mesh['batch'=8,'seq'=4,'mp'=8] {'batch','seq'}, dimensions={1} | all-to-all | bytes 393216 | tf_op jit(solution)/shard_map/all_to_all | solution.py:26
  60.4 0.1 copy.11
  60.5 0.1 broadcast_in_dim.3
  60.6 57.5 %all_to_all.42 = bf16[8,512,192]{1,2,0:T(8,128)(2,1)S(1)} all-to-all(bf16[8,512,192]{1,2,0:T(8,128)(2,1)S(1)} %broadcast_in_dim.3), channel_id=1, replica_groups=mesh['batch'=8,'seq'=4,'mp'=8] {'mp'}, dimensions={0} | all-to-all | bytes 3145728 | tf_op jit(solution)/shard_map/all_to_all | solution.py:15
  118.2 2.4 %copy.12 = bf16[8,512,192]{2,1,0:T(8,128)(2,1)} copy(bf16[8,512,192]{1,2,0:T(8,128)(2,1)S(1)} %all_to_all.42) | data formatting | bytes 3145728 | tf_op jit(solution)/shard_map/all_to_all | solution.py:15
  120.6 0.0 reduce-scatter.2.cloned.1.call-done
  120.6 1.7 convert_element_type.3
  122.3 57.6 %all-gather.2.cloned.1.call-done = bf16[4096,768]{1,0:T(8,128)(2,1)} async-done(((bf16[128,768]{1,0:T(8,128)(2,1)}), bf16[4096,768]{1,0:T(8,128)(2,1)}) %all-gather.2.cloned.1.call-update) | async-done | bytes 6291472 | tf_op jit(solution)/shard_map/all_gather | solution.py:30
  179.9 5.7 %fusion.2 = f32[192,768]{1,0:T(8,128)} fusion(bf16[8,32,16,192]{3,2,1,0:T(8,128)(2,1)} %bitcast.14, bf16[32,8,16,768]{3,2,1,0:T(8,128)(2,1)} %bitcast.18), kind=kOutput, calls=%fused_computation.2 | convolution fusion | flops 1207959552 | bytes 8454144 | tf_op jit(solution)/shard_map/dot_general | solution.py:34
Async XLA Ops:
  8.0 9.3 %copy-start = (bf16[128,768]{1,0:T(8,128)(2,1)S(1)}, bf16[128,768]{1,0:T(8,128)(2,1)}, u32[]{:S(2)}) copy-start(bf16[128,768]{1,0:T(8,128)(2,1)} %param.3) | copy-start | bytes 589828
  8.0 112.6 %reduce-scatter.2.cloned.1.call-start = ((), (), s32[]{:S(2)}) async-start(), calls=%async_computation.5 | async-start | bytes 3538944 | tf_op jit(solution)/shard_map/reduce_scatter | solution.py:43
  16.7 163.2 %all-gather.2.cloned.1.call-start = ((), (), s32[]{:S(2)}) async-start(), calls=%async_computation.4 | async-start | bytes 6488064 | tf_op jit(solution)/shard_map/all_gather | solution.py:30
Sparse Core Ops, SparseCore 0:
  16.8 84.8 reduce-scatter.1
Sparse Core Ops, SparseCore 1:
  20.6 159.2 all-gather.1
where the time goes:
time: 193 us
  blocking collectives  100 us (52%)
  waiting for transfers between devices  58.1 us (30%)
  between operations  15.5 us (8%)
  matrix products  14.3 us (7%)
  local copies, waits for them, and re-layouts  3.13 us (2%)
    all_gather x1, waiting for transfers between devices, shards(): lax.all_gather(cotangent, ('batch', 'seq'), axis=0, tiled=True)  57.6 us
    all_to_all x1, blocking collectives, copy_for_each(): return lax.all_to_all(copies, axis, split_axis=0, concat_axis=0, tiled=True)  57.5 us
    all_to_all x1, blocking collectives, shards(): lax.all_to_all(split_rows, ('batch', 'seq'), split_axis=1, concat_axis=0,...  28.9 us
    all_to_all x1, blocking collectives, shards(): lax.all_to_all(context, 'mp', split_axis=0, concat_axis=1, tiled=True)  13.7 us
    dot_general x1, matrix products, shards(): lax.dot_general(cotangent, out_weight, (((1,), (1,)), ((), ())), preferre...  8.62 us
    dot_general x1, matrix products, shards(): lax.dot_general(shaped_context, shaped_cotangent, (((0, 1, 2), (1, 0, 2))...  5.66 us
  transfers between devices with their start and end apart: 2, of which 1 were waited for; matrix products, arithmetic and copies ran while one was open for 2% of the time, Pallas kernels for 0%

commit v1 on v0

--- a/solution.py
+++ b/solution.py
@@ -2,6 +2,7 @@
 import jax.numpy as jnp
 from jax import lax
 from jax.sharding import PartitionSpec as P
+from jax.lax import all_to_all, axis_size
 
 
 def joined_along(blocks, dim):
@@ -27,7 +28,10 @@
         split_rows, ("batch", "seq"), split_axis=1, concat_axis=0, tiled=True
     )
     feature_block = gathered_copies(block_rows, "mp", 0)
-    all_cotangent = lax.all_gather(cotangent, ("batch", "seq"), axis=0, tiled=True)
+    opened = axis_size(("batch", "seq"))
+    e_now = jnp.stack(opened * [cotangent])
+    part_next = all_to_all(e_now, ("batch", "seq"), 0, 0)
+    all_cotangent = jnp.concatenate(part_next, axis=0)
     share = split_rows.shape[0]
     shaped_context = feature_block.reshape(members, groups, share, feature_block.shape[1])
     shaped_cotangent = all_cotangent.reshape(groups, members, share, all_cotangent.shape[1])

time: 193 us -> 283 us (1.47); the launches traced: 193 us -> 280 us
  waiting for transfers between devices: 58.1 us -> 158 us
  blocking collectives: 100 us -> 80.8 us
  starting transfers between devices: 0.08 us -> 4.94 us
  local copies, waits for them, and re-layouts: 3.13 us -> 6.53 us
    reduce_scatter x1, waiting for transfers between devices: 0.01 us -> 106 us  [shards(): lax.psum_scatter(partial_input, 'mp', scatter_dimension=1, tiled=True)]
    all_gather x1 -> x0, waiting for transfers between devices: 57.6 us -> none  [shards(): lax.all_gather(cotangent, ('batch', 'seq'), axis=0, tiled=True)]
    all_to_all x0 -> x1, waiting for transfers between devices: none -> 51.7 us  [shards(): part_next = all_to_all(e_now, ('batch', 'seq'), 0, 0)]
    all_to_all x1, blocking collectives: 57.5 us -> 43.8 us  [copy_for_each(): return lax.all_to_all(copies, axis, split_axis=0, concat_axis=0, tiled=True)]
    all_to_all x1, blocking collectives: 28.9 us -> 22.9 us  [shards(): lax.all_to_all(split_rows, ('batch', 'seq'), split_axis=1, concat_axis=0,...]
    all_to_all x0 -> x1, starting transfers between devices: none -> 4.89 us  [shards(): part_next = all_to_all(e_now, ('batch', 'seq'), 0, 0)]
    another operation x0 -> x1, local copies, waits for them, and re-layouts: none -> 3.37 us  [shards(): e_now = jnp.stack(opened * [cotangent])]
  transfers between devices with their start and end apart: 2 -> 2, of which waited for: 1 -> 2; matrix products, arithmetic and copies ran while one was open for 2% -> 4% of each run, Pallas kernels for 0% -> 0%
where the time goes in v1:
time: 283 us; the launch traced here: 280 us
  waiting for transfers between devices  158 us (56%)
  blocking collectives  80.8 us (29%)
  matrix products  14.1 us (5%)
  between operations  14.1 us (5%)
  local copies, waits for them, and re-layouts  6.53 us (2%)
  starting transfers between devices  4.94 us (2%)
    reduce_scatter x1, waiting for transfers between devices, shards(): lax.psum_scatter(partial_input, 'mp', scatter_dimension=1, tiled=True)  106 us
    all_to_all x1, waiting for transfers between devices, shards(): part_next = all_to_all(e_now, ('batch', 'seq'), 0, 0)  51.7 us
    all_to_all x1, blocking collectives, copy_for_each(): return lax.all_to_all(copies, axis, split_axis=0, concat_axis=0, tiled=True)  43.8 us
    all_to_all x1, blocking collectives, shards(): lax.all_to_all(split_rows, ('batch', 'seq'), split_axis=1, concat_axis=0,...  22.9 us
    all_to_all x1, blocking collectives, shards(): lax.all_to_all(context, 'mp', split_axis=0, concat_axis=1, tiled=True)  14.1 us
    dot_general x1, matrix products, shards(): lax.dot_general(cotangent, out_weight, (((1,), (1,)), ((), ())), preferre...  8.41 us
  transfers between devices with their start and end apart: 2, of which 2 were waited for; matrix products, arithmetic and copies ran while one was open for 4% of the time, Pallas kernels for 0%

profile of v1, /device:TPU:1, one launch (start us, length us, event | category | flops | bytes accessed | tf_op | source)
XLA Modules:
  0.0 279.8 jit_solution(12579087317526395054)
XLA Ops:
  7.2 0.0 copy-start
  7.2 14.1 %all_to_all.45 = bf16[8,16,768]{2,1,0:T(8,128)(2,1)S(1)} all-to-all(bf16[8,16,768]{2,1,0:T(8,128)(2,1)} %bitcast.17), channel_id=1, replica_groups=mesh['batch'=8,'seq'=4,'mp'=8] {'mp'}, dimensions={0} | all-to-all | bytes 393216 | tf_op jit(solution)/shard_map/all_to_all | solution.py:26
  21.2 0.1 copy.12
  21.3 0.3 all_to_all.35
  21.6 0.2 copy.13
  21.7 22.9 %all_to_all.46 = bf16[16,32,192]{2,0,1:T(8,128)(2,1)S(1)} all-to-all(bf16[16,32,192]{2,0,1:T(8,128)(2,1)S(1)} %copy.13), channel_id=1, replica_groups=mesh['batch'=8,'seq'=4,'mp'=8] {'batch','seq'}, dimensions={1} | all-to-all | bytes 393216 | tf_op jit(solution)/shard_map/all_to_all | solution.py:27
  44.7 0.1 copy.14
  44.8 0.1 broadcast_in_dim.3
  44.9 43.8 %all_to_all.47 = bf16[8,512,192]{1,2,0:T(8,128)(2,1)S(1)} all-to-all(bf16[8,512,192]{1,2,0:T(8,128)(2,1)S(1)} %broadcast_in_dim.3), channel_id=1, replica_groups=mesh['batch'=8,'seq'=4,'mp'=8] {'mp'}, dimensions={0} | all-to-all | bytes 3145728 | tf_op jit(solution)/shard_map/all_to_all | solution.py:16
  88.7 0.0 copy-done
  88.7 3.4 %stack.2 = bf16[32,128,768]{2,1,0:T(8,128)(2,1)} broadcast(bf16[128,768]{1,0:T(8,128)(2,1)S(1)} %copy-done), dimensions={1,2} | broadcast | bytes 6488064 | tf_op jit(solution)/shard_map/stack | solution.py:32
  92.1 4.9 %all-to-all-start.3 = ((bf16[32,128,768]{2,1,0:T(8,128)(2,1)}), bf16[32,128,768]{2,1,0:T(8,128)(2,1)}, u32[]{:S(2)}, u32[]{:S(2)}) async-start(bf16[32,128,768]{2,1,0:T(8,128)(2,1)} %stack.2), calls=%async_computation.3 | async-start | bytes 12582912 | tf_op jit(solution)/shard_map/all_to_all | solution.py:33
  97.0 0.0 reduce-scatter.2.cloned.1.call-start
  97.0 8.4 %fusion.5 = f32[128,6144]{1,0:T(8,128)} fusion(bf16[128,768]{1,0:T(8,128)(2,1)S(1)} %copy-done, bf16[6144,768]{1,0:T(8,128)(2,1)} %param.5), kind=kOutput, calls=%fused_computation.3 | convolution fusion | flops 1207959552 | bytes 12779520 | tf_op jit(solution)/shard_map/dot_general | solution.py:44
  105.5 0.0 reduce-scatter.2.cloned.1.call-update
  105.5 2.4 copy.15
  107.9 106.0 %reduce-scatter.2.cloned.1.call-done = f32[128,768]{1,0:T(8,128)} async-done(((f32[128,6144]{1,0:T(8,128)}), f32[128,768]{1,0:T(8,128)}) %reduce-scatter.2.cloned.1.call-update) | async-done | bytes 393232 | tf_op jit(solution)/shard_map/reduce_scatter | solution.py:47
  213.9 1.7 convert_element_type.3
  215.6 51.7 %all-to-all-done.3 = bf16[32,128,768]{2,1,0:T(8,128)(2,1)} async-done(((bf16[32,128,768]{2,1,0:T(8,128)(2,1)}), bf16[32,128,768]{2,1,0:T(8,128)(2,1)}, u32[]{:S(2)}, u32[]{:S(2)}) %all-to-all-start.3) | async-done | bytes 6291488 | tf_op jit(solution)/shard_map/all_to_all | solution.py:33
  267.3 5.7 %fusion.2 = f32[192,768]{1,0:T(8,128)} fusion(bf16[8,32,16,192]{3,2,1,0:T(8,128)(2,1)} %bitcast.14, bf16[32,8,16,768]{3,2,1,0:T(8,128)(2,1)} %bitcast.5), kind=kOutput, calls=%fused_computation.2 | convolution fusion | flops 1207959552 | bytes 8454144 | tf_op jit(solution)/shard_map/dot_general | solution.py:38
Async XLA Ops:
  7.2 81.6 %copy-start = (bf16[128,768]{1,0:T(8,128)(2,1)S(1)}, bf16[128,768]{1,0:T(8,128)(2,1)}, u32[]{:S(2)}) copy-start(bf16[128,768]{1,0:T(8,128)(2,1)} %param.4) | copy-start | bytes 589828
  92.1 175.2 %all-to-all-start.3 = ((bf16[32,128,768]{2,1,0:T(8,128)(2,1)}), bf16[32,128,768]{2,1,0:T(8,128)(2,1)}, u32[]{:S(2)}, u32[]{:S(2)}) async-start(bf16[32,128,768]{2,1,0:T(8,128)(2,1)} %stack.2), calls=%async_computation.3 | async-start | bytes 12582912 | tf_op jit(solution)/shard_map/all_to_all | solution.py:33
  97.0 116.9 %reduce-scatter.2.cloned.1.call-start = ((), (), s32[]{:S(2)}) async-start(), calls=%async_computation.5 | async-start | bytes 3538944 | tf_op jit(solution)/shard_map/reduce_scatter | solution.py:47
Sparse Core Ops, SparseCore 0:
  105.6 108.2 reduce-scatter.1
